TPU v7x, 128 devices: a whole 4x4x4 slice. The times are simulated.
128 devices in a mesh: prow: 8 (over y, core), pcol: 16 (over z, x).
Axes of the slice: x: 4, y: 4, z: 4, core: 2. Of those that a mesh axis runs over, the one named last changes fastest.
Arguments:
- inverse_cov: bfloat16 [8192, 8192], P('prow', 'pcol'), may hold values from -0.5 to 4.5, as said below
- cosines: float32 [8192, 8192], P('prow', 'pcol'), may hold values from -1 to 1, as said below
- sky_maps: bfloat16 [8192, 192], P('pcol'), may hold values from -6 to 6
Outputs:
- filtered: bfloat16 [8192, 192], P('prow')
- spectra: float32 [64, 192], replicated
Inputs may be any that keep to these rules, and one draw needn't show every extreme that they name: `inverse_cov`: symmetric, with a dominant diagonal. `cosines`: symmetric.
All inputs are finite; a program needn't handle non-finite values.
Results may differ from a plain program's by a relative error of at most 0.0033.
Values may be sent and summed in bfloat16 or wider, within the bound.
No kernel may reach another device: no remote copies, remote signals or barrier semaphores. Data moves between devices by JAX's collectives and lax.ppermute only.
A program may use at most 64 MiB of HBM per device.

v0:
```python
import jax
import jax.numpy as jnp
from jax import lax
from jax.sharding import Mesh
from jax.sharding import PartitionSpec as P

NPIX = 8192
L = 64
LMIN = 2
GROUP = 4
PCOL = ("pcol_0", "pcol_1")
PROW = ("prow_0", "prow_1")
PROW_PCOL = ("prow_0", "prow_1", "pcol_0", "pcol_1")


def split_up(value, dim, length):
    dims = value.shape
    parts = value.reshape(*dims[:dim], length, dims[dim] // length, *dims[dim + 1 :])
    return jnp.moveaxis(parts, dim, 0)


def summed_on_arrival(value, axis, dim):
    length = lax.axis_size(axis)
    parts = lax.all_to_all(split_up(value, dim, length), axis, 0, 0, tiled=True)
    return jnp.sum(parts, axis=0)


def from_everyone(value, axis):
    length = lax.axis_size(axis)
    return lax.all_to_all(
        jnp.broadcast_to(value[None], (length, *value.shape)), axis, 0, 0, tiled=True
    )


def joined_along(parts, dim):
    parts = jnp.moveaxis(parts, 0, dim)
    dims = parts.shape
    return parts.reshape(*dims[:dim], dims[dim] * dims[dim + 1], *dims[dim + 2 :])


def collect(value, axis, dim):
    parts = from_everyone(value, axis)
    return joined_along(parts, dim)


def broadcast(value, axis, root):
    return lax.dynamic_index_in_dim(lax.all_gather(value, axis), root, 0, keepdims=False)


def by_axis(value, axes):
    for axis in axes:
        value = lax.psum(value, axis)
    return value


def next_legendre(previous, current, cosine, degree):
    return ((2.0 * degree - 1.0) * cosine * current - (degree - 1.0) * previous) / degree


def per_device(inverse_cov, cosines, sky_maps):
    cols_here = inverse_cov.shape[1]
    own_rows = summed_on_arrival(
        jnp.dot(inverse_cov, sky_maps, preferred_element_type=jnp.float32), PCOL, 0
    ).astype(jnp.bfloat16)
    filtered = collect(own_rows, PCOL, 0)
    column_index = lax.axis_index(PCOL)
    col_ratio = lax.axis_size(PCOL) // lax.axis_size(PROW)
    owner_row = column_index // col_ratio
    source = broadcast(filtered, PROW, owner_row)
    filtered_cols = lax.dynamic_slice_in_dim(
        source, column_index % col_ratio * cols_here, cols_here, 0
    )
    rows_f32 = filtered.astype(jnp.float32)
    previous = jnp.ones_like(cosines)
    current = cosines

    def advance(carried, turn_index):
        previous, current = carried
        term_list = []
        weights = []
        for offset in range(GROUP):
            degree = (LMIN + turn_index * GROUP + offset).astype(jnp.float32)
            next_term = next_legendre(previous, current, cosines, degree)
            term_list.append(next_term.astype(jnp.bfloat16))
            weights.append((2.0 * degree + 1.0) / NPIX)
            previous, current = (current, next_term)
        stacked = jnp.stack(term_list)
        product = jnp.einsum(
            "grc,cm->grm", stacked, filtered_cols, preferred_element_type=jnp.float32
        )
        quadratic = jnp.sum(product * rows_f32[None], axis=1)
        return ((previous, current), quadratic * jnp.stack(weights)[:, None])

    carried, partial_spectra = lax.scan(
        advance, (previous, current), jnp.arange(L // GROUP, dtype=jnp.int32)
    )
    spectra = by_axis(partial_spectra.reshape(L, -1), PROW_PCOL)
    return (filtered, spectra)


def solution(mesh):
    split = Mesh(mesh.devices.reshape(4, 2, 4, 4), ("prow_0", "prow_1", "pcol_0", "pcol_1"))
    placed = (P(PROW, PCOL), P(PROW, PCOL), P(PCOL, None))
    return jax.shard_map(
        per_device, mesh=split, in_specs=placed, out_specs=(P(PROW, None), P()), check_vma=False
    )
```

profile of v0, /device:TPU:0, one launch (start us, length us, event | category | flops | bytes accessed | tf_op | source)
XLA Modules:
  0.0 353.4 jit_solution(7335706579062819510)
XLA Ops:
  9.8 24.9 %all_to_all.10 = f32[16,64,192]{2,1,0:T(8,128)S(1)} all-to-all(f32[16,64,192]{2,1,0:T(8,128)S(1)} %bitcast.57), channel_id=1, replica_groups=mesh['prow_0'=4,'prow_1'=2,'pcol_0'=4,'pcol_1'=4] {'pcol_0','pcol_1'}, dimensions={0} | all-to-all | bytes 1572864 | tf_op jit(solution)/shard_map/all_to_all | solution.py:24
  34.8 13.7 %all_to_all.11 = bf16[16,64,192]{2,1,0:T(8,128)(2,1)S(1)} all-to-all(bf16[16,64,192]{2,1,0:T(8,128)(2,1)S(1)} %broadcast_in_dim.7), channel_id=1, replica_groups=mesh['prow_0'=4,'prow_1'=2,'pcol_0'=4,'pcol_1'=4] {'pcol_0','pcol_1'}, dimensions={0} | all-to-all | bytes 786432 | tf_op jit(solution)/shard_map/all_to_all | solution.py:30
  55.3 19.7 %all-gather.2.cloned.1.call-done = bf16[8,1024,192]{1,2,0:T(8,128)(2,1)} async-done(((bf16[1,1024,192]{1,2,0:T(8,128)(2,1)}), bf16[8,1024,192]{1,2,0:T(8,128)(2,1)}) %all-gather.2.cloned.1.call-update) | async-done | bytes 3145744 | tf_op jit(solution)/shard_map/all_gather | solution.py:47
  76.1 214.6 %while.18 = (s32[]{:T(128)}, f32[1024,512]{1,0:T(8,128)}, f32[1024,512]{1,0:T(8,128)S(1)}, f32[16,4,192]{2,1,0:T(4,128)S(1)}, s32[16]{0:T(128)S(1)}, /*index=5*/...) while((s32[]{:T(128)}, f32[1024,512]{1,0:T(8,128)}, ...), condition=%wide.region_3.4_spmd.clone, body=%wide.region_1.3_spmd.clone.sunk | while | flops 832045056 | bytes 69153048 | solution.py:94
  90.4 4.2 %convert_bitcast_fusion.6 = (bf16[1,1024,512]{2,1,0:T(8,128)(2,1)S(1)}, f32[1024,512]{1,0:T(8,128)S(1)}, bf16[1,1024,512]{2,1,0:T(8,128)(2,1)S(1)}) fusion(f32[]{:T(128)} %bitcast.47, f32[]{:T(128)S(6)} %sub.103, f32[]{:T(128)} %bitcast.48, f32[1024,512]{1,0:T(8,128)} %copy-done.2, f32[]{:T(128)S(6)} %sub.104, f32[]{:T(128)} %bitcast.49, ...), kind=kLoop, calls=%fused_computation.16.clone.1 | loop fusion | flops 9437184 | bytes 10485797 | tf_op jit(solution)/shard_map/while/body/eval_jaxpr/stack | solution.py:87
  94.6 4.1 %convert_bitcast_fusion.7 = (bf16[1,1024,512]{2,1,0:T(8,128)(2,1)S(1)}, f32[1024,512]{1,0:T(8,128)}, bf16[1,1024,512]{2,1,0:T(8,128)(2,1)S(1)}) fusion(f32[]{:T(128)} %bitcast.50, f32[]{:T(128)} %bitcast.48, f32[1024,512]{1,0:T(8,128)} %copy-done.2, f32[]{:T(128)S(6)} %sub.104, f32[]{:T(128)} %bitcast.49, f32[1024,512]{1,0:T(8,128)S(1)} %copy-done.5, ...), kind=kLoop, calls=%fused_computation.15.clone.1 | loop fusion | flops 9437184 | bytes 12582949 | tf_op jit(solution)/shard_map/while/body/eval_jaxpr/stack | solution.py:87
  103.8 4.2 %convert_bitcast_fusion.6 = (bf16[1,1024,512]{2,1,0:T(8,128)(2,1)S(1)}, f32[1024,512]{1,0:T(8,128)S(1)}, bf16[1,1024,512]{2,1,0:T(8,128)(2,1)S(1)}) fusion(f32[]{:T(128)} %bitcast.47, f32[]{:T(128)S(6)} %sub.103, f32[]{:T(128)} %bitcast.48, f32[1024,512]{1,0:T(8,128)} %copy-done.2, f32[]{:T(128)S(6)} %sub.104, f32[]{:T(128)} %bitcast.49, ...), kind=kLoop, calls=%fused_computation.16.clone.1 | loop fusion | flops 9437184 | bytes 10485797 | tf_op jit(solution)/shard_map/while/body/eval_jaxpr/stack | solution.py:87
  108.0 4.1 %convert_bitcast_fusion.7 = (bf16[1,1024,512]{2,1,0:T(8,128)(2,1)S(1)}, f32[1024,512]{1,0:T(8,128)}, bf16[1,1024,512]{2,1,0:T(8,128)(2,1)S(1)}) fusion(f32[]{:T(128)} %bitcast.50, f32[]{:T(128)} %bitcast.48, f32[1024,512]{1,0:T(8,128)} %copy-done.2, f32[]{:T(128)S(6)} %sub.104, f32[]{:T(128)} %bitcast.49, f32[1024,512]{1,0:T(8,128)S(1)} %copy-done.5, ...), kind=kLoop, calls=%fused_computation.15.clone.1 | loop fusion | flops 9437184 | bytes 12582949 | tf_op jit(solution)/shard_map/while/body/eval_jaxpr/stack | solution.py:87
  117.3 4.2 %convert_bitcast_fusion.6 = (bf16[1,1024,512]{2,1,0:T(8,128)(2,1)S(1)}, f32[1024,512]{1,0:T(8,128)S(1)}, bf16[1,1024,512]{2,1,0:T(8,128)(2,1)S(1)}) fusion(f32[]{:T(128)} %bitcast.47, f32[]{:T(128)S(6)} %sub.103, f32[]{:T(128)} %bitcast.48, f32[1024,512]{1,0:T(8,128)} %copy-done.2, f32[]{:T(128)S(6)} %sub.104, f32[]{:T(128)} %bitcast.49, ...), kind=kLoop, calls=%fused_computation.16.clone.1 | loop fusion | flops 9437184 | bytes 10485797 | tf_op jit(solution)/shard_map/while/body/eval_jaxpr/stack | solution.py:87
  130.7 4.2 %convert_bitcast_fusion.6 = (bf16[1,1024,512]{2,1,0:T(8,128)(2,1)S(1)}, f32[1024,512]{1,0:T(8,128)S(1)}, bf16[1,1024,512]{2,1,0:T(8,128)(2,1)S(1)}) fusion(f32[]{:T(128)} %bitcast.47, f32[]{:T(128)S(6)} %sub.103, f32[]{:T(128)} %bitcast.48, f32[1024,512]{1,0:T(8,128)} %copy-done.2, f32[]{:T(128)S(6)} %sub.104, f32[]{:T(128)} %bitcast.49, ...), kind=kLoop, calls=%fused_computation.16.clone.1 | loop fusion | flops 9437184 | bytes 10485797 | tf_op jit(solution)/shard_map/while/body/eval_jaxpr/stack | solution.py:87
  144.2 4.2 %convert_bitcast_fusion.6 = (bf16[1,1024,512]{2,1,0:T(8,128)(2,1)S(1)}, f32[1024,512]{1,0:T(8,128)S(1)}, bf16[1,1024,512]{2,1,0:T(8,128)(2,1)S(1)}) fusion(f32[]{:T(128)} %bitcast.47, f32[]{:T(128)S(6)} %sub.103, f32[]{:T(128)} %bitcast.48, f32[1024,512]{1,0:T(8,128)} %copy-done.2, f32[]{:T(128)S(6)} %sub.104, f32[]{:T(128)} %bitcast.49, ...), kind=kLoop, calls=%fused_computation.16.clone.1 | loop fusion | flops 9437184 | bytes 10485797 | tf_op jit(solution)/shard_map/while/body/eval_jaxpr/stack | solution.py:87
  157.6 4.2 %convert_bitcast_fusion.6 = (bf16[1,1024,512]{2,1,0:T(8,128)(2,1)S(1)}, f32[1024,512]{1,0:T(8,128)S(1)}, bf16[1,1024,512]{2,1,0:T(8,128)(2,1)S(1)}) fusion(f32[]{:T(128)} %bitcast.47, f32[]{:T(128)S(6)} %sub.103, f32[]{:T(128)} %bitcast.48, f32[1024,512]{1,0:T(8,128)} %copy-done.2, f32[]{:T(128)S(6)} %sub.104, f32[]{:T(128)} %bitcast.49, ...), kind=kLoop, calls=%fused_computation.16.clone.1 | loop fusion | flops 9437184 | bytes 10485797 | tf_op jit(solution)/shard_map/while/body/eval_jaxpr/stack | solution.py:87
  171.1 4.2 %convert_bitcast_fusion.6 = (bf16[1,1024,512]{2,1,0:T(8,128)(2,1)S(1)}, f32[1024,512]{1,0:T(8,128)S(1)}, bf16[1,1024,512]{2,1,0:T(8,128)(2,1)S(1)}) fusion(f32[]{:T(128)} %bitcast.47, f32[]{:T(128)S(6)} %sub.103, f32[]{:T(128)} %bitcast.48, f32[1024,512]{1,0:T(8,128)} %copy-done.2, f32[]{:T(128)S(6)} %sub.104, f32[]{:T(128)} %bitcast.49, ...), kind=kLoop, calls=%fused_computation.16.clone.1 | loop fusion | flops 9437184 | bytes 10485797 | tf_op jit(solution)/shard_map/while/body/eval_jaxpr/stack | solution.py:87
  184.5 4.2 %convert_bitcast_fusion.6 = (bf16[1,1024,512]{2,1,0:T(8,128)(2,1)S(1)}, f32[1024,512]{1,0:T(8,128)S(1)}, bf16[1,1024,512]{2,1,0:T(8,128)(2,1)S(1)}) fusion(f32[]{:T(128)} %bitcast.47, f32[]{:T(128)S(6)} %sub.103, f32[]{:T(128)} %bitcast.48, f32[1024,512]{1,0:T(8,128)} %copy-done.2, f32[]{:T(128)S(6)} %sub.104, f32[]{:T(128)} %bitcast.49, ...), kind=kLoop, calls=%fused_computation.16.clone.1 | loop fusion | flops 9437184 | bytes 10485797 | tf_op jit(solution)/shard_map/while/body/eval_jaxpr/stack | solution.py:87
  198.0 4.2 %convert_bitcast_fusion.6 = (bf16[1,1024,512]{2,1,0:T(8,128)(2,1)S(1)}, f32[1024,512]{1,0:T(8,128)S(1)}, bf16[1,1024,512]{2,1,0:T(8,128)(2,1)S(1)}) fusion(f32[]{:T(128)} %bitcast.47, f32[]{:T(128)S(6)} %sub.103, f32[]{:T(128)} %bitcast.48, f32[1024,512]{1,0:T(8,128)} %copy-done.2, f32[]{:T(128)S(6)} %sub.104, f32[]{:T(128)} %bitcast.49, ...), kind=kLoop, calls=%fused_computation.16.clone.1 | loop fusion | flops 9437184 | bytes 10485797 | tf_op jit(solution)/shard_map/while/body/eval_jaxpr/stack | solution.py:87
  211.4 4.2 %convert_bitcast_fusion.6 = (bf16[1,1024,512]{2,1,0:T(8,128)(2,1)S(1)}, f32[1024,512]{1,0:T(8,128)S(1)}, bf16[1,1024,512]{2,1,0:T(8,128)(2,1)S(1)}) fusion(f32[]{:T(128)} %bitcast.47, f32[]{:T(128)S(6)} %sub.103, f32[]{:T(128)} %bitcast.48, f32[1024,512]{1,0:T(8,128)} %copy-done.2, f32[]{:T(128)S(6)} %sub.104, f32[]{:T(128)} %bitcast.49, ...), kind=kLoop, calls=%fused_computation.16.clone.1 | loop fusion | flops 9437184 | bytes 10485797 | tf_op jit(solution)/shard_map/while/body/eval_jaxpr/stack | solution.py:87
  224.9 4.2 %convert_bitcast_fusion.6 = (bf16[1,1024,512]{2,1,0:T(8,128)(2,1)S(1)}, f32[1024,512]{1,0:T(8,128)S(1)}, bf16[1,1024,512]{2,1,0:T(8,128)(2,1)S(1)}) fusion(f32[]{:T(128)} %bitcast.47, f32[]{:T(128)S(6)} %sub.103, f32[]{:T(128)} %bitcast.48, f32[1024,512]{1,0:T(8,128)} %copy-done.2, f32[]{:T(128)S(6)} %sub.104, f32[]{:T(128)} %bitcast.49, ...), kind=kLoop, calls=%fused_computation.16.clone.1 | loop fusion | flops 9437184 | bytes 10485797 | tf_op jit(solution)/shard_map/while/body/eval_jaxpr/stack | solution.py:87
  238.3 4.2 %convert_bitcast_fusion.6 = (bf16[1,1024,512]{2,1,0:T(8,128)(2,1)S(1)}, f32[1024,512]{1,0:T(8,128)S(1)}, bf16[1,1024,512]{2,1,0:T(8,128)(2,1)S(1)}) fusion(f32[]{:T(128)} %bitcast.47, f32[]{:T(128)S(6)} %sub.103, f32[]{:T(128)} %bitcast.48, f32[1024,512]{1,0:T(8,128)} %copy-done.2, f32[]{:T(128)S(6)} %sub.104, f32[]{:T(128)} %bitcast.49, ...), kind=kLoop, calls=%fused_computation.16.clone.1 | loop fusion | flops 9437184 | bytes 10485797 | tf_op jit(solution)/shard_map/while/body/eval_jaxpr/stack | solution.py:87
  251.8 4.2 %convert_bitcast_fusion.6 = (bf16[1,1024,512]{2,1,0:T(8,128)(2,1)S(1)}, f32[1024,512]{1,0:T(8,128)S(1)}, bf16[1,1024,512]{2,1,0:T(8,128)(2,1)S(1)}) fusion(f32[]{:T(128)} %bitcast.47, f32[]{:T(128)S(6)} %sub.103, f32[]{:T(128)} %bitcast.48, f32[1024,512]{1,0:T(8,128)} %copy-done.2, f32[]{:T(128)S(6)} %sub.104, f32[]{:T(128)} %bitcast.49, ...), kind=kLoop, calls=%fused_computation.16.clone.1 | loop fusion | flops 9437184 | bytes 10485797 | tf_op jit(solution)/shard_map/while/body/eval_jaxpr/stack | solution.py:87
  265.2 4.2 %convert_bitcast_fusion.6 = (bf16[1,1024,512]{2,1,0:T(8,128)(2,1)S(1)}, f32[1024,512]{1,0:T(8,128)S(1)}, bf16[1,1024,512]{2,1,0:T(8,128)(2,1)S(1)}) fusion(f32[]{:T(128)} %bitcast.47, f32[]{:T(128)S(6)} %sub.103, f32[]{:T(128)} %bitcast.48, f32[1024,512]{1,0:T(8,128)} %copy-done.2, f32[]{:T(128)S(6)} %sub.104, f32[]{:T(128)} %bitcast.49, ...), kind=kLoop, calls=%fused_computation.16.clone.1 | loop fusion | flops 9437184 | bytes 10485797 | tf_op jit(solution)/shard_map/while/body/eval_jaxpr/stack | solution.py:87
  278.6 4.2 %convert_bitcast_fusion.6 = (bf16[1,1024,512]{2,1,0:T(8,128)(2,1)S(1)}, f32[1024,512]{1,0:T(8,128)S(1)}, bf16[1,1024,512]{2,1,0:T(8,128)(2,1)S(1)}) fusion(f32[]{:T(128)} %bitcast.47, f32[]{:T(128)S(6)} %sub.103, f32[]{:T(128)} %bitcast.48, f32[1024,512]{1,0:T(8,128)} %copy-done.2, f32[]{:T(128)S(6)} %sub.104, f32[]{:T(128)} %bitcast.49, ...), kind=kLoop, calls=%fused_computation.16.clone.1 | loop fusion | flops 9437184 | bytes 10485797 | tf_op jit(solution)/shard_map/while/body/eval_jaxpr/stack | solution.py:87
  290.7 16.5 %psum.28 = f32[64,192]{1,0:T(8,128)S(1)} all-reduce(f32[64,192]{1,0:T(8,128)S(1)} %reshape.63), channel_id=1, replica_groups=mesh['prow_0'=4,'prow_1'=2,'pcol_0'=4,'pcol_1'=4] {'prow_0'}, use_global_device_ids=true, to_apply=%region_4.5 | all-reduce | flops 12288 | bytes 98304 | tf_op jit(solution)/shard_map/psum | solution.py:52
  310.8 17.7 %psum.30 = f32[64,192]{1,0:T(8,128)S(1)} all-reduce(f32[64,192]{1,0:T(8,128)S(1)} %psum.29), channel_id=1, replica_groups=mesh['prow_0'=4,'prow_1'=2,'pcol_0'=4,'pcol_1'=4] {'pcol_0'}, use_global_device_ids=true, to_apply=%region_6.7 | all-reduce | flops 12288 | bytes 98304 | tf_op jit(solution)/shard_map/psum | solution.py:52
  328.5 18.0 %psum.31 = f32[64,192]{1,0:T(8,128)} all-reduce(f32[64,192]{1,0:T(8,128)S(1)} %psum.30), channel_id=1, replica_groups=mesh['prow_0'=4,'prow_1'=2,'pcol_0'=4,'pcol_1'=4] {'pcol_1'}, use_global_device_ids=true, to_apply=%region_7.8 | all-reduce | flops 12288 | bytes 98304 | tf_op jit(solution)/shard_map/psum | solution.py:52
  (276 shorter events, 146.6 us)
Async XLA Ops:
  7.2 67.8 %all-gather.2.cloned.1.call-start = ((), (), s32[]{:S(2)}) async-start(), calls=%async_computation.2 | async-start | bytes 3538944 | tf_op jit(solution)/shard_map/all_gather | solution.py:47
  50.6 25.5 %copy-start.4 = (f32[1024,512]{1,0:T(8,128)S(1)}, f32[1024,512]{1,0:T(8,128)}, u32[]{:S(2)}) copy-start(f32[1024,512]{1,0:T(8,128)} %param.6) | copy-start | bytes 6291460
  90.4 4.2 %copy-start.1 = (f32[1024,512]{1,0:T(8,128)S(1)}, f32[1024,512]{1,0:T(8,128)}, u32[]{:S(2)}) copy-start(f32[1024,512]{1,0:T(8,128)} %get-tuple-element.322) | copy-start | bytes 6291460 | tf_op jit(solution)/shard_map/while
  90.4 4.2 %copy-start.5 = (f32[1024,512]{1,0:T(8,128)S(1)}, f32[1024,512]{1,0:T(8,128)}, u32[]{:S(2)}) copy-start(f32[1024,512]{1,0:T(8,128)} %get-tuple-element.300) | copy-start | bytes 6291460 | tf_op jit(solution)/shard_map/while
  103.8 4.2 %copy-start.1 = (f32[1024,512]{1,0:T(8,128)S(1)}, f32[1024,512]{1,0:T(8,128)}, u32[]{:S(2)}) copy-start(f32[1024,512]{1,0:T(8,128)} %get-tuple-element.322) | copy-start | bytes 6291460 | tf_op jit(solution)/shard_map/while
  103.8 4.2 %copy-start.5 = (f32[1024,512]{1,0:T(8,128)S(1)}, f32[1024,512]{1,0:T(8,128)}, u32[]{:S(2)}) copy-start(f32[1024,512]{1,0:T(8,128)} %get-tuple-element.300) | copy-start | bytes 6291460 | tf_op jit(solution)/shard_map/while
  117.3 4.2 %copy-start.1 = (f32[1024,512]{1,0:T(8,128)S(1)}, f32[1024,512]{1,0:T(8,128)}, u32[]{:S(2)}) copy-start(f32[1024,512]{1,0:T(8,128)} %get-tuple-element.322) | copy-start | bytes 6291460 | tf_op jit(solution)/shard_map/while
  117.3 4.2 %copy-start.5 = (f32[1024,512]{1,0:T(8,128)S(1)}, f32[1024,512]{1,0:T(8,128)}, u32[]{:S(2)}) copy-start(f32[1024,512]{1,0:T(8,128)} %get-tuple-element.300) | copy-start | bytes 6291460 | tf_op jit(solution)/shard_map/while
  130.7 4.2 %copy-start.1 = (f32[1024,512]{1,0:T(8,128)S(1)}, f32[1024,512]{1,0:T(8,128)}, u32[]{:S(2)}) copy-start(f32[1024,512]{1,0:T(8,128)} %get-tuple-element.322) | copy-start | bytes 6291460 | tf_op jit(solution)/shard_map/while
  130.7 4.2 %copy-start.5 = (f32[1024,512]{1,0:T(8,128)S(1)}, f32[1024,512]{1,0:T(8,128)}, u32[]{:S(2)}) copy-start(f32[1024,512]{1,0:T(8,128)} %get-tuple-element.300) | copy-start | bytes 6291460 | tf_op jit(solution)/shard_map/while
  144.2 4.2 %copy-start.1 = (f32[1024,512]{1,0:T(8,128)S(1)}, f32[1024,512]{1,0:T(8,128)}, u32[]{:S(2)}) copy-start(f32[1024,512]{1,0:T(8,128)} %get-tuple-element.322) | copy-start | bytes 6291460 | tf_op jit(solution)/shard_map/while
  144.2 4.2 %copy-start.5 = (f32[1024,512]{1,0:T(8,128)S(1)}, f32[1024,512]{1,0:T(8,128)}, u32[]{:S(2)}) copy-start(f32[1024,512]{1,0:T(8,128)} %get-tuple-element.300) | copy-start | bytes 6291460 | tf_op jit(solution)/shard_map/while
  157.6 4.2 %copy-start.1 = (f32[1024,512]{1,0:T(8,128)S(1)}, f32[1024,512]{1,0:T(8,128)}, u32[]{:S(2)}) copy-start(f32[1024,512]{1,0:T(8,128)} %get-tuple-element.322) | copy-start | bytes 6291460 | tf_op jit(solution)/shard_map/while
  157.6 4.2 %copy-start.5 = (f32[1024,512]{1,0:T(8,128)S(1)}, f32[1024,512]{1,0:T(8,128)}, u32[]{:S(2)}) copy-start(f32[1024,512]{1,0:T(8,128)} %get-tuple-element.300) | copy-start | bytes 6291460 | tf_op jit(solution)/shard_map/while
  171.1 4.2 %copy-start.1 = (f32[1024,512]{1,0:T(8,128)S(1)}, f32[1024,512]{1,0:T(8,128)}, u32[]{:S(2)}) copy-start(f32[1024,512]{1,0:T(8,128)} %get-tuple-element.322) | copy-start | bytes 6291460 | tf_op jit(solution)/shard_map/while
  171.1 4.2 %copy-start.5 = (f32[1024,512]{1,0:T(8,128)S(1)}, f32[1024,512]{1,0:T(8,128)}, u32[]{:S(2)}) copy-start(f32[1024,512]{1,0:T(8,128)} %get-tuple-element.300) | copy-start | bytes 6291460 | tf_op jit(solution)/shard_map/while
  184.5 4.2 %copy-start.5 = (f32[1024,512]{1,0:T(8,128)S(1)}, f32[1024,512]{1,0:T(8,128)}, u32[]{:S(2)}) copy-start(f32[1024,512]{1,0:T(8,128)} %get-tuple-element.300) | copy-start | bytes 6291460 | tf_op jit(solution)/shard_map/while
  198.0 4.2 %copy-start.5 = (f32[1024,512]{1,0:T(8,128)S(1)}, f32[1024,512]{1,0:T(8,128)}, u32[]{:S(2)}) copy-start(f32[1024,512]{1,0:T(8,128)} %get-tuple-element.300) | copy-start | bytes 6291460 | tf_op jit(solution)/shard_map/while
  211.4 4.2 %copy-start.5 = (f32[1024,512]{1,0:T(8,128)S(1)}, f32[1024,512]{1,0:T(8,128)}, u32[]{:S(2)}) copy-start(f32[1024,512]{1,0:T(8,128)} %get-tuple-element.300) | copy-start | bytes 6291460 | tf_op jit(solution)/shard_map/while
  224.8 4.2 %copy-start.5 = (f32[1024,512]{1,0:T(8,128)S(1)}, f32[1024,512]{1,0:T(8,128)}, u32[]{:S(2)}) copy-start(f32[1024,512]{1,0:T(8,128)} %get-tuple-element.300) | copy-start | bytes 6291460 | tf_op jit(solution)/shard_map/while
  238.3 4.2 %copy-start.5 = (f32[1024,512]{1,0:T(8,128)S(1)}, f32[1024,512]{1,0:T(8,128)}, u32[]{:S(2)}) copy-start(f32[1024,512]{1,0:T(8,128)} %get-tuple-element.300) | copy-start | bytes 6291460 | tf_op jit(solution)/shard_map/while
  251.7 4.2 %copy-start.5 = (f32[1024,512]{1,0:T(8,128)S(1)}, f32[1024,512]{1,0:T(8,128)}, u32[]{:S(2)}) copy-start(f32[1024,512]{1,0:T(8,128)} %get-tuple-element.300) | copy-start | bytes 6291460 | tf_op jit(solution)/shard_map/while
  265.2 4.2 %copy-start.5 = (f32[1024,512]{1,0:T(8,128)S(1)}, f32[1024,512]{1,0:T(8,128)}, u32[]{:S(2)}) copy-start(f32[1024,512]{1,0:T(8,128)} %get-tuple-element.300) | copy-start | bytes 6291460 | tf_op jit(solution)/shard_map/while
  278.6 4.2 %copy-start.5 = (f32[1024,512]{1,0:T(8,128)S(1)}, f32[1024,512]{1,0:T(8,128)}, u32[]{:S(2)}) copy-start(f32[1024,512]{1,0:T(8,128)} %get-tuple-element.300) | copy-start | bytes 6291460 | tf_op jit(solution)/shard_map/while
  (60 other events, 124.6 us)
Sparse Core Ops, SparseCore 0:
  49.7 25.3 all-gather.1
where the time goes:
time: 355 us; the launch traced here: 353 us
  other arithmetic  137 us (39%)
  blocking collectives  94.5 us (27%)
  local copies, waits for them, and re-layouts  44.7 us (13%)
  matrix products  32 us (9%)
  waiting for transfers between devices  19.8 us (6%)
  between operations  14.2 us (4%)
  loops' own time  11.1 us (3%)
    another operation x32, other arithmetic, advance(): stacked = jnp.stack(term_list)  132 us
    psum x4, blocking collectives, by_axis(): value = lax.psum(value, axis)  55.8 us
    dot_general x16, matrix products, advance(): jnp.einsum('grc,cm->grm', stacked, filtered_cols, preferred_element_type=...  30.6 us
    while x176, local copies, waits for them, and re-layouts  27.1 us
    all_to_all x1, blocking collectives, summed_on_arrival(): parts = lax.all_to_all(split_up(value, dim, length), axis, 0, 0, tiled=True)  24.9 us
    all_gather x1, waiting for transfers between devices, broadcast(): lax.all_gather(value, axis)  19.7 us
    all_to_all x1, blocking collectives, from_everyone(): lax.all_to_all(jnp.broadcast_to(value[None], (length, *value.shape)), axi...  13.7 us
    another operation x1, loops' own time, per_device(): lax.scan(advance, (previous, current), jnp.arange(L // GROUP, dtype=jnp.i...  11.1 us
  transfers between devices with their start and end apart: 1, of which 1 were waited for; matrix products, arithmetic and copies ran while one was open for 2% of the time, Pallas kernels for 0%

commit v1 on v0

--- a/solution.py
+++ b/solution.py
@@ -49,7 +49,7 @@
 
 def by_axis(value, axes):
     for axis in axes:
-        value = lax.psum(value, axis)
+        value = lax.all_gather(value, axis).sum(axis=0)
     return value
 
 

time: 355 us -> 340 us (0.958)
  blocking collectives: 94.5 us -> 78.4 us
    psum x4 -> x0, blocking collectives: 55.8 us -> none  [by_axis(): value = lax.psum(value, axis)]
    all_gather x0 -> x4, blocking collectives: none -> 39.7 us  [by_axis(): value = lax.all_gather(value, axis).sum(axis=0)]
where the time goes in v1:
time: 340 us; the launch traced here: 338 us
  other arithmetic  138 us (41%)
  blocking collectives  78.4 us (23%)
  local copies, waits for them, and re-layouts  44.7 us (13%)
  matrix products  32 us (9%)
  waiting for transfers between devices  19.8 us (6%)
  between operations  14.2 us (4%)
  loops' own time  11.1 us (3%)
    another operation x32, other arithmetic, advance(): stacked = jnp.stack(term_list)  132 us
    all_gather x4, blocking collectives, by_axis(): value = lax.all_gather(value, axis).sum(axis=0)  39.7 us
    dot_general x16, matrix products, advance(): jnp.einsum('grc,cm->grm', stacked, filtered_cols, preferred_element_type=...  30.6 us
    while x176, local copies, waits for them, and re-layouts  27.1 us
    all_to_all x1, blocking collectives, summed_on_arrival(): parts = lax.all_to_all(split_up(value, dim, length), axis, 0, 0, tiled=True)  24.9 us
    all_gather x1, waiting for transfers between devices, broadcast(): lax.all_gather(value, axis)  19.7 us
    all_to_all x1, blocking collectives, from_everyone(): lax.all_to_all(jnp.broadcast_to(value[None], (length, *value.shape)), axi...  13.7 us
    another operation x1, loops' own time, per_device(): lax.scan(advance, (previous, current), jnp.arange(L // GROUP, dtype=jnp.i...  11.1 us
  transfers between devices with their start and end apart: 1, of which 1 were waited for; matrix products, arithmetic and copies ran while one was open for 2% of the time, Pallas kernels for 0%

profile of v1, /device:TPU:0, one launch (start us, length us, event | category | flops | bytes accessed | tf_op | source)
XLA Modules:
  0.0 337.9 jit_solution(14711332085989907678)
XLA Ops:
  9.8 24.9 %all_to_all.10 = f32[16,64,192]{2,1,0:T(8,128)S(1)} all-to-all(f32[16,64,192]{2,1,0:T(8,128)S(1)} %bitcast.60), channel_id=1, replica_groups=mesh['prow_0'=4,'prow_1'=2,'pcol_0'=4,'pcol_1'=4] {'pcol_0','pcol_1'}, dimensions={0} | all-to-all | bytes 1572864 | tf_op jit(solution)/shard_map/all_to_all | solution.py:24
  34.8 13.7 %all_to_all.11 = bf16[16,64,192]{2,1,0:T(8,128)(2,1)S(1)} all-to-all(bf16[16,64,192]{2,1,0:T(8,128)(2,1)S(1)} %broadcast_in_dim.7), channel_id=1, replica_groups=mesh['prow_0'=4,'prow_1'=2,'pcol_0'=4,'pcol_1'=4] {'pcol_0','pcol_1'}, dimensions={0} | all-to-all | bytes 786432 | tf_op jit(solution)/shard_map/all_to_all | solution.py:30
  55.3 19.7 %all-gather.5.cloned.1.call-done = bf16[8,1024,192]{1,2,0:T(8,128)(2,1)} async-done(((bf16[1,1024,192]{1,2,0:T(8,128)(2,1)}), bf16[8,1024,192]{1,2,0:T(8,128)(2,1)}) %all-gather.5.cloned.1.call-update) | async-done | bytes 3145744 | tf_op jit(solution)/shard_map/all_gather | solution.py:47
  76.1 214.6 %while.18 = (s32[]{:T(128)}, f32[1024,512]{1,0:T(8,128)}, f32[1024,512]{1,0:T(8,128)S(1)}, f32[16,4,192]{2,1,0:T(4,128)S(1)}, s32[16]{0:T(128)S(1)}, /*index=5*/...) while((s32[]{:T(128)}, f32[1024,512]{1,0:T(8,128)}, ...), condition=%wide.region_3.4_spmd.clone, body=%wide.region_1.3_spmd.clone.sunk | while | flops 832045056 | bytes 69153048 | solution.py:94
  81.1 4.1 %convert_bitcast_fusion.7 = (bf16[1,1024,512]{2,1,0:T(8,128)(2,1)S(1)}, f32[1024,512]{1,0:T(8,128)}, bf16[1,1024,512]{2,1,0:T(8,128)(2,1)S(1)}) fusion(f32[]{:T(128)} %bitcast.53, f32[]{:T(128)} %bitcast.51, f32[1024,512]{1,0:T(8,128)} %copy-done.2, f32[]{:T(128)S(6)} %sub.104, f32[]{:T(128)} %bitcast.52, f32[1024,512]{1,0:T(8,128)S(1)} %copy-done.5, ...), kind=kLoop, calls=%fused_computation.15.clone.1 | loop fusion | flops 9437184 | bytes 12582949 | tf_op jit(solution)/shard_map/while/body/eval_jaxpr/stack | solution.py:87
  90.4 4.2 %convert_bitcast_fusion.6 = (bf16[1,1024,512]{2,1,0:T(8,128)(2,1)S(1)}, f32[1024,512]{1,0:T(8,128)S(1)}, bf16[1,1024,512]{2,1,0:T(8,128)(2,1)S(1)}) fusion(f32[]{:T(128)} %bitcast.50, f32[]{:T(128)S(6)} %sub.103, f32[]{:T(128)} %bitcast.51, f32[1024,512]{1,0:T(8,128)} %copy-done.2, f32[]{:T(128)S(6)} %sub.104, f32[]{:T(128)} %bitcast.52, ...), kind=kLoop, calls=%fused_computation.16.clone.1 | loop fusion | flops 9437184 | bytes 10485797 | tf_op jit(solution)/shard_map/while/body/eval_jaxpr/stack | solution.py:87
  94.6 4.1 %convert_bitcast_fusion.7 = (bf16[1,1024,512]{2,1,0:T(8,128)(2,1)S(1)}, f32[1024,512]{1,0:T(8,128)}, bf16[1,1024,512]{2,1,0:T(8,128)(2,1)S(1)}) fusion(f32[]{:T(128)} %bitcast.53, f32[]{:T(128)} %bitcast.51, f32[1024,512]{1,0:T(8,128)} %copy-done.2, f32[]{:T(128)S(6)} %sub.104, f32[]{:T(128)} %bitcast.52, f32[1024,512]{1,0:T(8,128)S(1)} %copy-done.5, ...), kind=kLoop, calls=%fused_computation.15.clone.1 | loop fusion | flops 9437184 | bytes 12582949 | tf_op jit(solution)/shard_map/while/body/eval_jaxpr/stack | solution.py:87
  103.8 4.2 %convert_bitcast_fusion.6 = (bf16[1,1024,512]{2,1,0:T(8,128)(2,1)S(1)}, f32[1024,512]{1,0:T(8,128)S(1)}, bf16[1,1024,512]{2,1,0:T(8,128)(2,1)S(1)}) fusion(f32[]{:T(128)} %bitcast.50, f32[]{:T(128)S(6)} %sub.103, f32[]{:T(128)} %bitcast.51, f32[1024,512]{1,0:T(8,128)} %copy-done.2, f32[]{:T(128)S(6)} %sub.104, f32[]{:T(128)} %bitcast.52, ...), kind=kLoop, calls=%fused_computation.16.clone.1 | loop fusion | flops 9437184 | bytes 10485797 | tf_op jit(solution)/shard_map/while/body/eval_jaxpr/stack | solution.py:87
  117.3 4.2 %convert_bitcast_fusion.6 = (bf16[1,1024,512]{2,1,0:T(8,128)(2,1)S(1)}, f32[1024,512]{1,0:T(8,128)S(1)}, bf16[1,1024,512]{2,1,0:T(8,128)(2,1)S(1)}) fusion(f32[]{:T(128)} %bitcast.50, f32[]{:T(128)S(6)} %sub.103, f32[]{:T(128)} %bitcast.51, f32[1024,512]{1,0:T(8,128)} %copy-done.2, f32[]{:T(128)S(6)} %sub.104, f32[]{:T(128)} %bitcast.52, ...), kind=kLoop, calls=%fused_computation.16.clone.1 | loop fusion | flops 9437184 | bytes 10485797 | tf_op jit(solution)/shard_map/while/body/eval_jaxpr/stack | solution.py:87
  130.7 4.2 %convert_bitcast_fusion.6 = (bf16[1,1024,512]{2,1,0:T(8,128)(2,1)S(1)}, f32[1024,512]{1,0:T(8,128)S(1)}, bf16[1,1024,512]{2,1,0:T(8,128)(2,1)S(1)}) fusion(f32[]{:T(128)} %bitcast.50, f32[]{:T(128)S(6)} %sub.103, f32[]{:T(128)} %bitcast.51, f32[1024,512]{1,0:T(8,128)} %copy-done.2, f32[]{:T(128)S(6)} %sub.104, f32[]{:T(128)} %bitcast.52, ...), kind=kLoop, calls=%fused_computation.16.clone.1 | loop fusion | flops 9437184 | bytes 10485797 | tf_op jit(solution)/shard_map/while/body/eval_jaxpr/stack | solution.py:87
  144.2 4.2 %convert_bitcast_fusion.6 = (bf16[1,1024,512]{2,1,0:T(8,128)(2,1)S(1)}, f32[1024,512]{1,0:T(8,128)S(1)}, bf16[1,1024,512]{2,1,0:T(8,128)(2,1)S(1)}) fusion(f32[]{:T(128)} %bitcast.50, f32[]{:T(128)S(6)} %sub.103, f32[]{:T(128)} %bitcast.51, f32[1024,512]{1,0:T(8,128)} %copy-done.2, f32[]{:T(128)S(6)} %sub.104, f32[]{:T(128)} %bitcast.52, ...), kind=kLoop, calls=%fused_computation.16.clone.1 | loop fusion | flops 9437184 | bytes 10485797 | tf_op jit(solution)/shard_map/while/body/eval_jaxpr/stack | solution.py:87
  157.6 4.2 %convert_bitcast_fusion.6 = (bf16[1,1024,512]{2,1,0:T(8,128)(2,1)S(1)}, f32[1024,512]{1,0:T(8,128)S(1)}, bf16[1,1024,512]{2,1,0:T(8,128)(2,1)S(1)}) fusion(f32[]{:T(128)} %bitcast.50, f32[]{:T(128)S(6)} %sub.103, f32[]{:T(128)} %bitcast.51, f32[1024,512]{1,0:T(8,128)} %copy-done.2, f32[]{:T(128)S(6)} %sub.104, f32[]{:T(128)} %bitcast.52, ...), kind=kLoop, calls=%fused_computation.16.clone.1 | loop fusion | flops 9437184 | bytes 10485797 | tf_op jit(solution)/shard_map/while/body/eval_jaxpr/stack | solution.py:87
  171.1 4.2 %convert_bitcast_fusion.6 = (bf16[1,1024,512]{2,1,0:T(8,128)(2,1)S(1)}, f32[1024,512]{1,0:T(8,128)S(1)}, bf16[1,1024,512]{2,1,0:T(8,128)(2,1)S(1)}) fusion(f32[]{:T(128)} %bitcast.50, f32[]{:T(128)S(6)} %sub.103, f32[]{:T(128)} %bitcast.51, f32[1024,512]{1,0:T(8,128)} %copy-done.2, f32[]{:T(128)S(6)} %sub.104, f32[]{:T(128)} %bitcast.52, ...), kind=kLoop, calls=%fused_computation.16.clone.1 | loop fusion | flops 9437184 | bytes 10485797 | tf_op jit(solution)/shard_map/while/body/eval_jaxpr/stack | solution.py:87
  184.5 4.2 %convert_bitcast_fusion.6 = (bf16[1,1024,512]{2,1,0:T(8,128)(2,1)S(1)}, f32[1024,512]{1,0:T(8,128)S(1)}, bf16[1,1024,512]{2,1,0:T(8,128)(2,1)S(1)}) fusion(f32[]{:T(128)} %bitcast.50, f32[]{:T(128)S(6)} %sub.103, f32[]{:T(128)} %bitcast.51, f32[1024,512]{1,0:T(8,128)} %copy-done.2, f32[]{:T(128)S(6)} %sub.104, f32[]{:T(128)} %bitcast.52, ...), kind=kLoop, calls=%fused_computation.16.clone.1 | loop fusion | flops 9437184 | bytes 10485797 | tf_op jit(solution)/shard_map/while/body/eval_jaxpr/stack | solution.py:87
  198.0 4.2 %convert_bitcast_fusion.6 = (bf16[1,1024,512]{2,1,0:T(8,128)(2,1)S(1)}, f32[1024,512]{1,0:T(8,128)S(1)}, bf16[1,1024,512]{2,1,0:T(8,128)(2,1)S(1)}) fusion(f32[]{:T(128)} %bitcast.50, f32[]{:T(128)S(6)} %sub.103, f32[]{:T(128)} %bitcast.51, f32[1024,512]{1,0:T(8,128)} %copy-done.2, f32[]{:T(128)S(6)} %sub.104, f32[]{:T(128)} %bitcast.52, ...), kind=kLoop, calls=%fused_computation.16.clone.1 | loop fusion | flops 9437184 | bytes 10485797 | tf_op jit(solution)/shard_map/while/body/eval_jaxpr/stack | solution.py:87
  211.4 4.2 %convert_bitcast_fusion.6 = (bf16[1,1024,512]{2,1,0:T(8,128)(2,1)S(1)}, f32[1024,512]{1,0:T(8,128)S(1)}, bf16[1,1024,512]{2,1,0:T(8,128)(2,1)S(1)}) fusion(f32[]{:T(128)} %bitcast.50, f32[]{:T(128)S(6)} %sub.103, f32[]{:T(128)} %bitcast.51, f32[1024,512]{1,0:T(8,128)} %copy-done.2, f32[]{:T(128)S(6)} %sub.104, f32[]{:T(128)} %bitcast.52, ...), kind=kLoop, calls=%fused_computation.16.clone.1 | loop fusion | flops 9437184 | bytes 10485797 | tf_op jit(solution)/shard_map/while/body/eval_jaxpr/stack | solution.py:87
  224.9 4.2 %convert_bitcast_fusion.6 = (bf16[1,1024,512]{2,1,0:T(8,128)(2,1)S(1)}, f32[1024,512]{1,0:T(8,128)S(1)}, bf16[1,1024,512]{2,1,0:T(8,128)(2,1)S(1)}) fusion(f32[]{:T(128)} %bitcast.50, f32[]{:T(128)S(6)} %sub.103, f32[]{:T(128)} %bitcast.51, f32[1024,512]{1,0:T(8,128)} %copy-done.2, f32[]{:T(128)S(6)} %sub.104, f32[]{:T(128)} %bitcast.52, ...), kind=kLoop, calls=%fused_computation.16.clone.1 | loop fusion | flops 9437184 | bytes 10485797 | tf_op jit(solution)/shard_map/while/body/eval_jaxpr/stack | solution.py:87
  238.3 4.2 %convert_bitcast_fusion.6 = (bf16[1,1024,512]{2,1,0:T(8,128)(2,1)S(1)}, f32[1024,512]{1,0:T(8,128)S(1)}, bf16[1,1024,512]{2,1,0:T(8,128)(2,1)S(1)}) fusion(f32[]{:T(128)} %bitcast.50, f32[]{:T(128)S(6)} %sub.103, f32[]{:T(128)} %bitcast.51, f32[1024,512]{1,0:T(8,128)} %copy-done.2, f32[]{:T(128)S(6)} %sub.104, f32[]{:T(128)} %bitcast.52, ...), kind=kLoop, calls=%fused_computation.16.clone.1 | loop fusion | flops 9437184 | bytes 10485797 | tf_op jit(solution)/shard_map/while/body/eval_jaxpr/stack | solution.py:87
  251.8 4.2 %convert_bitcast_fusion.6 = (bf16[1,1024,512]{2,1,0:T(8,128)(2,1)S(1)}, f32[1024,512]{1,0:T(8,128)S(1)}, bf16[1,1024,512]{2,1,0:T(8,128)(2,1)S(1)}) fusion(f32[]{:T(128)} %bitcast.50, f32[]{:T(128)S(6)} %sub.103, f32[]{:T(128)} %bitcast.51, f32[1024,512]{1,0:T(8,128)} %copy-done.2, f32[]{:T(128)S(6)} %sub.104, f32[]{:T(128)} %bitcast.52, ...), kind=kLoop, calls=%fused_computation.16.clone.1 | loop fusion | flops 9437184 | bytes 10485797 | tf_op jit(solution)/shard_map/while/body/eval_jaxpr/stack | solution.py:87
  265.2 4.2 %convert_bitcast_fusion.6 = (bf16[1,1024,512]{2,1,0:T(8,128)(2,1)S(1)}, f32[1024,512]{1,0:T(8,128)S(1)}, bf16[1,1024,512]{2,1,0:T(8,128)(2,1)S(1)}) fusion(f32[]{:T(128)} %bitcast.50, f32[]{:T(128)S(6)} %sub.103, f32[]{:T(128)} %bitcast.51, f32[1024,512]{1,0:T(8,128)} %copy-done.2, f32[]{:T(128)S(6)} %sub.104, f32[]{:T(128)} %bitcast.52, ...), kind=kLoop, calls=%fused_computation.16.clone.1 | loop fusion | flops 9437184 | bytes 10485797 | tf_op jit(solution)/shard_map/while/body/eval_jaxpr/stack | solution.py:87
  278.6 4.2 %convert_bitcast_fusion.6 = (bf16[1,1024,512]{2,1,0:T(8,128)(2,1)S(1)}, f32[1024,512]{1,0:T(8,128)S(1)}, bf16[1,1024,512]{2,1,0:T(8,128)(2,1)S(1)}) fusion(f32[]{:T(128)} %bitcast.50, f32[]{:T(128)S(6)} %sub.103, f32[]{:T(128)} %bitcast.51, f32[1024,512]{1,0:T(8,128)} %copy-done.2, f32[]{:T(128)S(6)} %sub.104, f32[]{:T(128)} %bitcast.52, ...), kind=kLoop, calls=%fused_computation.16.clone.1 | loop fusion | flops 9437184 | bytes 10485797 | tf_op jit(solution)/shard_map/while/body/eval_jaxpr/stack | solution.py:87
  290.7 12.3 %all_gather.25 = f32[4,64,192]{2,1,0:T(8,128)S(1)} all-gather(f32[1,64,192]{2,1,0:T(8,128)S(1)} %all_gather_reshape.7), channel_id=1, replica_groups=mesh['prow_0'=4,'prow_1'=2,'pcol_0'=4,'pcol_1'=4] {'prow_0'}, dimensions={0}, use_global_device_ids=true | all-gather | bytes 245760 | tf_op jit(solution)/shard_map/all_gather | solution.py:52
  304.9 12.7 %all-gather.1 = f32[256,192]{1,0:T(8,128)S(1)} all-gather(f32[64,192]{1,0:T(8,128)S(1)} %reduce_sum.62), channel_id=3, replica_groups=mesh['prow_0'=4,'prow_1'=2,'pcol_0'=4,'pcol_1'=4] {'pcol_0'}, dimensions={0}, use_global_device_ids=true | all-gather | bytes 245760 | tf_op jit(solution)/shard_map/all_gather | solution.py:52
  317.7 12.8 %all-gather.2 = f32[256,192]{1,0:T(8,128)S(1)} all-gather(f32[64,192]{1,0:T(8,128)S(1)} %reduce_sum.63), channel_id=4, replica_groups=mesh['prow_0'=4,'prow_1'=2,'pcol_0'=4,'pcol_1'=4] {'pcol_1'}, dimensions={0}, use_global_device_ids=true | all-gather | bytes 245760 | tf_op jit(solution)/shard_map/all_gather | solution.py:52
  (280 shorter events, 145.6 us)
Async XLA Ops:
  7.2 67.8 %all-gather.5.cloned.1.call-start = ((), (), s32[]{:S(2)}) async-start(), calls=%async_computation.2 | async-start | bytes 3538944 | tf_op jit(solution)/shard_map/all_gather | solution.py:47
  50.6 25.5 %copy-start.4 = (f32[1024,512]{1,0:T(8,128)S(1)}, f32[1024,512]{1,0:T(8,128)}, u32[]{:S(2)}) copy-start(f32[1024,512]{1,0:T(8,128)} %param.6) | copy-start | bytes 6291460
  90.4 4.2 %copy-start.1 = (f32[1024,512]{1,0:T(8,128)S(1)}, f32[1024,512]{1,0:T(8,128)}, u32[]{:S(2)}) copy-start(f32[1024,512]{1,0:T(8,128)} %get-tuple-element.332) | copy-start | bytes 6291460 | tf_op jit(solution)/shard_map/while
  90.4 4.2 %copy-start.5 = (f32[1024,512]{1,0:T(8,128)S(1)}, f32[1024,512]{1,0:T(8,128)}, u32[]{:S(2)}) copy-start(f32[1024,512]{1,0:T(8,128)} %get-tuple-element.310) | copy-start | bytes 6291460 | tf_op jit(solution)/shard_map/while
  103.8 4.2 %copy-start.1 = (f32[1024,512]{1,0:T(8,128)S(1)}, f32[1024,512]{1,0:T(8,128)}, u32[]{:S(2)}) copy-start(f32[1024,512]{1,0:T(8,128)} %get-tuple-element.332) | copy-start | bytes 6291460 | tf_op jit(solution)/shard_map/while
  103.8 4.2 %copy-start.5 = (f32[1024,512]{1,0:T(8,128)S(1)}, f32[1024,512]{1,0:T(8,128)}, u32[]{:S(2)}) copy-start(f32[1024,512]{1,0:T(8,128)} %get-tuple-element.310) | copy-start | bytes 6291460 | tf_op jit(solution)/shard_map/while
  117.3 4.2 %copy-start.1 = (f32[1024,512]{1,0:T(8,128)S(1)}, f32[1024,512]{1,0:T(8,128)}, u32[]{:S(2)}) copy-start(f32[1024,512]{1,0:T(8,128)} %get-tuple-element.332) | copy-start | bytes 6291460 | tf_op jit(solution)/shard_map/while
  117.3 4.2 %copy-start.5 = (f32[1024,512]{1,0:T(8,128)S(1)}, f32[1024,512]{1,0:T(8,128)}, u32[]{:S(2)}) copy-start(f32[1024,512]{1,0:T(8,128)} %get-tuple-element.310) | copy-start | bytes 6291460 | tf_op jit(solution)/shard_map/while
  130.7 4.2 %copy-start.1 = (f32[1024,512]{1,0:T(8,128)S(1)}, f32[1024,512]{1,0:T(8,128)}, u32[]{:S(2)}) copy-start(f32[1024,512]{1,0:T(8,128)} %get-tuple-element.332) | copy-start | bytes 6291460 | tf_op jit(solution)/shard_map/while
  130.7 4.2 %copy-start.5 = (f32[1024,512]{1,0:T(8,128)S(1)}, f32[1024,512]{1,0:T(8,128)}, u32[]{:S(2)}) copy-start(f32[1024,512]{1,0:T(8,128)} %get-tuple-element.310) | copy-start | bytes 6291460 | tf_op jit(solution)/shard_map/while
  144.2 4.2 %copy-start.1 = (f32[1024,512]{1,0:T(8,128)S(1)}, f32[1024,512]{1,0:T(8,128)}, u32[]{:S(2)}) copy-start(f32[1024,512]{1,0:T(8,128)} %get-tuple-element.332) | copy-start | bytes 6291460 | tf_op jit(solution)/shard_map/while
  144.2 4.2 %copy-start.5 = (f32[1024,512]{1,0:T(8,128)S(1)}, f32[1024,512]{1,0:T(8,128)}, u32[]{:S(2)}) copy-start(f32[1024,512]{1,0:T(8,128)} %get-tuple-element.310) | copy-start | bytes 6291460 | tf_op jit(solution)/shard_map/while
  157.6 4.2 %copy-start.1 = (f32[1024,512]{1,0:T(8,128)S(1)}, f32[1024,512]{1,0:T(8,128)}, u32[]{:S(2)}) copy-start(f32[1024,512]{1,0:T(8,128)} %get-tuple-element.332) | copy-start | bytes 6291460 | tf_op jit(solution)/shard_map/while
  157.6 4.2 %copy-start.5 = (f32[1024,512]{1,0:T(8,128)S(1)}, f32[1024,512]{1,0:T(8,128)}, u32[]{:S(2)}) copy-start(f32[1024,512]{1,0:T(8,128)} %get-tuple-element.310) | copy-start | bytes 6291460 | tf_op jit(solution)/shard_map/while
  171.1 4.2 %copy-start.1 = (f32[1024,512]{1,0:T(8,128)S(1)}, f32[1024,512]{1,0:T(8,128)}, u32[]{:S(2)}) copy-start(f32[1024,512]{1,0:T(8,128)} %get-tuple-element.332) | copy-start | bytes 6291460 | tf_op jit(solution)/shard_map/while
  171.1 4.2 %copy-start.5 = (f32[1024,512]{1,0:T(8,128)S(1)}, f32[1024,512]{1,0:T(8,128)}, u32[]{:S(2)}) copy-start(f32[1024,512]{1,0:T(8,128)} %get-tuple-element.310) | copy-start | bytes 6291460 | tf_op jit(solution)/shard_map/while
  184.5 4.2 %copy-start.5 = (f32[1024,512]{1,0:T(8,128)S(1)}, f32[1024,512]{1,0:T(8,128)}, u32[]{:S(2)}) copy-start(f32[1024,512]{1,0:T(8,128)} %get-tuple-element.310) | copy-start | bytes 6291460 | tf_op jit(solution)/shard_map/while
  198.0 4.2 %copy-start.5 = (f32[1024,512]{1,0:T(8,128)S(1)}, f32[1024,512]{1,0:T(8,128)}, u32[]{:S(2)}) copy-start(f32[1024,512]{1,0:T(8,128)} %get-tuple-element.310) | copy-start | bytes 6291460 | tf_op jit(solution)/shard_map/while
  211.4 4.2 %copy-start.5 = (f32[1024,512]{1,0:T(8,128)S(1)}, f32[1024,512]{1,0:T(8,128)}, u32[]{:S(2)}) copy-start(f32[1024,512]{1,0:T(8,128)} %get-tuple-element.310) | copy-start | bytes 6291460 | tf_op jit(solution)/shard_map/while
  224.8 4.2 %copy-start.5 = (f32[1024,512]{1,0:T(8,128)S(1)}, f32[1024,512]{1,0:T(8,128)}, u32[]{:S(2)}) copy-start(f32[1024,512]{1,0:T(8,128)} %get-tuple-element.310) | copy-start | bytes 6291460 | tf_op jit(solution)/shard_map/while
  238.3 4.2 %copy-start.5 = (f32[1024,512]{1,0:T(8,128)S(1)}, f32[1024,512]{1,0:T(8,128)}, u32[]{:S(2)}) copy-start(f32[1024,512]{1,0:T(8,128)} %get-tuple-element.310) | copy-start | bytes 6291460 | tf_op jit(solution)/shard_map/while
  251.7 4.2 %copy-start.5 = (f32[1024,512]{1,0:T(8,128)S(1)}, f32[1024,512]{1,0:T(8,128)}, u32[]{:S(2)}) copy-start(f32[1024,512]{1,0:T(8,128)} %get-tuple-element.310) | copy-start | bytes 6291460 | tf_op jit(solution)/shard_map/while
  265.2 4.2 %copy-start.5 = (f32[1024,512]{1,0:T(8,128)S(1)}, f32[1024,512]{1,0:T(8,128)}, u32[]{:S(2)}) copy-start(f32[1024,512]{1,0:T(8,128)} %get-tuple-element.310) | copy-start | bytes 6291460 | tf_op jit(solution)/shard_map/while
  278.6 4.2 %copy-start.5 = (f32[1024,512]{1,0:T(8,128)S(1)}, f32[1024,512]{1,0:T(8,128)}, u32[]{:S(2)}) copy-start(f32[1024,512]{1,0:T(8,128)} %get-tuple-element.310) | copy-start | bytes 6291460 | tf_op jit(solution)/shard_map/while
  (60 other events, 124.6 us)
Sparse Core Ops, SparseCore 0:
  49.7 25.3 all-gather.4
